TPU v7x, 32 devices: a whole 2x2x4 slice. The times are simulated.
32 devices in a mesh: len: 2 (over x), wid: 4 (over z), dep: 4 (over y, core).
Axes of the slice: x: 2, y: 2, z: 4, core: 2. Of those that a mesh axis runs over, the one named last changes fastest.
Arguments:
- coords: float32 [3, 32768], P(None, ('len', 'wid', 'dep')), may hold values from -3 to 3
- velocity: float32 [3, 32768], P(None, ('len', 'wid', 'dep')), may hold values from -6 to 6
- node_mass: float32 [32768], P(('len', 'wid', 'dep')), may hold values from 0.5 to 2
- corner_nodes: int32 [4, 32768], P(None, ('len', 'wid', 'dep')), may hold values from 0 to 1151, as said below
- shape_grad: float32 [8, 32768], P(None, ('len', 'wid', 'dep')), may hold values from -5 to 5
- frame_angles: float32 [2, 32768], P(None, ('len', 'wid', 'dep')), may hold values from -3.140625 to 3.140625
- volume: float32 [32768], P(('len', 'wid', 'dep')), may hold values from 0.5 to 2
- stress: float32 [3, 32768], P(None, ('len', 'wid', 'dep')), may hold values from -5 to 5
- send_nodes: int32 [32, 16, 256], P(('len', 'wid', 'dep')), may hold values from 0 to 1023
- tile_count: int32 [32], P(('len', 'wid', 'dep')), may hold values from 1 to 4, as said below
- tile_nodes: int32 [128, 128], P(('len', 'wid', 'dep')), may hold values from 0 to 4095
- tile_facets: int32 [4, 128, 128], P(None, ('len', 'wid', 'dep')), may hold values from 0 to 4095
- pair_mask: int32 [128, 128, 128], P(('len', 'wid', 'dep')), may hold values 0 or 1
Outputs:
- coords_out: float32 [3, 32768], P(None, ('len', 'wid', 'dep'))
- velocity_out: float32 [3, 32768], P(None, ('len', 'wid', 'dep'))
- stress_out: float32 [3, 32768], P(None, ('len', 'wid', 'dep'))
Inputs may be any that keep to these rules, and one draw needn't show every extreme that they name: `corner_nodes`: for the element at device-local position i (i = e mod 1024), every entry lies from (i // 128) * 128 to (i // 128) * 128 + 2 * 128 - 1. An entry j below 1024 names the element device's own node j; an entry 1024 + i names node i of the next device in the order len, wid, dep, the last device's next being the first. `send_nodes`: entry [p, g, k] is a node of device p, by its local number, sent to device g of p's slab; nodes may repeat. `tile_count`: some device has 4 live tiles in every draw; a device's tiles at and past its count are not used. `tile_nodes`: slot g * 256 + k of the tile's device is slot k of what device g of its slab sends it. `tile_facets`: slots as for tile_nodes, one for each of a facet's four corners.
All inputs are finite; a program needn't handle non-finite values. No bound on the sum of `pair_mask` on one device may be relied on, other than what follows from the above.
Results may differ from a plain program's by a relative error of at most 0.0003.
Values sent between devices are 32-bit elements; how exact they have to be, the bound alone decides.
A program may use at most 64 MiB of HBM per device.

v0:
```python
import math

import jax
import jax.numpy as jnp
from jax import lax
from jax.sharding import PartitionSpec as P

RIM = 128
STEPS = 2


TIME_STEP = 0.1
YOUNG_MOD = 1.0
POISSON = 0.3
HOURGLASS = 0.1
RADIUS_SQ = 1.0
STIFFNESS = 0.1
DAMPING = 0.05


def from_behind(value, axis, steps):
    count = lax.axis_size(axis)
    pairs = [(source, (source + steps) % count) for source in range(count)]
    return lax.ppermute(value, axis, pairs)


def frame_vectors(frame_angles):
    polar_angle = frame_angles[0]
    azimuth = frame_angles[1]
    axis_one = jnp.stack(
        [
            jnp.cos(polar_angle) * jnp.cos(azimuth),
            jnp.cos(polar_angle) * jnp.sin(azimuth),
            -jnp.sin(polar_angle),
        ]
    )
    axis_two = jnp.stack([-jnp.sin(azimuth), jnp.cos(azimuth), jnp.zeros_like(azimuth)])
    return (axis_one, axis_two)


def element_forces(corner_vel, shape_grad, axis_one, axis_two, volume, stress):
    grad_x = shape_grad[:4]
    grad_y = shape_grad[4:]
    along_one = jnp.sum(axis_one[:, None, :] * corner_vel, axis=0)
    along_two = jnp.sum(axis_two[:, None, :] * corner_vel, axis=0)
    rate_xx = jnp.sum(grad_x * along_one, axis=0)
    rate_yy = jnp.sum(grad_y * along_two, axis=0)
    rate_xy = jnp.sum(grad_y * along_one + grad_x * along_two, axis=0)
    factor = TIME_STEP * YOUNG_MOD / (1.0 - POISSON * POISSON)
    sigma_xx = stress[0] + factor * (rate_xx + POISSON * rate_yy)
    sigma_yy = stress[1] + factor * (POISSON * rate_xx + rate_yy)
    sigma_xy = stress[2] + factor * 0.5 * (1.0 - POISSON) * rate_xy
    hourglass_mode = jnp.array([1.0, -1.0, 1.0, -1.0], jnp.float32)[:, None]
    hourglass_rate = jnp.sum(hourglass_mode[None] * corner_vel, axis=1)
    force_one = -volume * (grad_x * sigma_xx + grad_y * sigma_xy)
    force_two = -volume * (grad_y * sigma_yy + grad_x * sigma_xy)
    corner_force = (
        axis_one[:, None] * force_one[None]
        + axis_two[:, None] * force_two[None]
        - HOURGLASS * volume * hourglass_mode[None] * hourglass_rate[:, None]
    )
    return (corner_force, jnp.stack([sigma_xx, sigma_yy, sigma_xy]))


def tile_forces(node_coordinates, node_velocities, corner_pos, corner_vel, pair_bits, live_row):
    facet_centroid = 0.25 * jnp.sum(corner_pos, axis=1)
    centroid_velocity = 0.25 * jnp.sum(corner_vel, axis=1)
    inner_product = jnp.einsum(
        "ywq,ywk->wqk", node_coordinates, facet_centroid, precision=lax.Precision.HIGHEST
    )
    distance = (
        jnp.sum(node_coordinates * node_coordinates, axis=0)[:, :, None]
        + jnp.sum(facet_centroid * facet_centroid, axis=0)[:, None, :]
        - 2.0 * inner_product
    )
    corner_weight = (
        pair_bits.astype(jnp.float32)
        * live_row[:, None, None]
        * jnp.maximum(RADIUS_SQ - distance, 0.0)
    )
    row_sum = jnp.sum(corner_weight, axis=2)
    col_sum = jnp.sum(corner_weight, axis=1)
    gathered_positions = jnp.einsum(
        "yml,mjl->ymj", facet_centroid, corner_weight, precision=lax.Precision.HIGHEST
    )
    gathered_velocities = jnp.einsum(
        "yml,mjl->ymj", centroid_velocity, corner_weight, precision=lax.Precision.HIGHEST
    )
    node_force = STIFFNESS * (row_sum * node_coordinates - gathered_positions) - DAMPING * (
        row_sum * node_velocities - gathered_velocities
    )
    outgoing_positions = jnp.einsum(
        "ewo,woj->ewj", node_coordinates, corner_weight, precision=lax.Precision.HIGHEST
    )
    outgoing_velocities = jnp.einsum(
        "ewo,woj->ewj", node_velocities, corner_weight, precision=lax.Precision.HIGHEST
    )
    facet_force = STIFFNESS * (outgoing_positions - col_sum * facet_centroid) - DAMPING * (
        outgoing_velocities - col_sum * centroid_velocity
    )
    return (node_force, -0.25 * facet_force)


def split_parts(values):
    first = lax.optimization_barrier(values.astype(jnp.bfloat16))
    rest = values - first.astype(jnp.float32)
    second = lax.optimization_barrier(rest.astype(jnp.bfloat16))
    third = (rest - second.astype(jnp.float32)).astype(jnp.bfloat16)
    return jnp.concatenate([first, second, third], axis=0)


def put_rows(values, index, total):
    chans, count = values.shape
    low_span = math.gcd(total, 128)
    high_span = total // low_span
    block = math.gcd(count, 1024)
    turns = count // block
    parts = jnp.transpose(split_parts(values).reshape(3 * chans, turns, block), (1, 0, 2))
    index_blocks = index.reshape(turns, block)
    low_iota = jnp.arange(low_span, dtype=jnp.int32)
    high_iota = jnp.arange(high_span, dtype=jnp.int32)

    def add_block(running, pieces):
        part, ids = pieces
        low_match = ids[:, None] % low_span == low_iota[None, :]
        spread_rows = jnp.where(low_match[None], part[:, :, None], jnp.zeros((), jnp.bfloat16))
        high_match = (ids[:, None] // low_span == high_iota[None, :]).astype(jnp.bfloat16)
        return (
            running
            + jnp.einsum(
                "mh,kml->khl", high_match, spread_rows, preferred_element_type=jnp.float32
            ),
            None,
        )

    summed, unused = lax.scan(
        add_block, jnp.zeros((3 * chans, high_span, low_span), jnp.float32), (parts, index_blocks)
    )
    return summed.reshape(3, chans, total).sum(axis=0)


def window_layout(corner_nodes, span):
    elements = corner_nodes.shape[1]
    blocks = elements // span
    group = math.gcd(blocks, 8)
    rounds = blocks // group
    starts = (jnp.arange(blocks, dtype=jnp.int32) * span)[None, :, None]
    local_ids = (corner_nodes.reshape(4, blocks, span) - starts).reshape(4, rounds, group, span)
    return (jnp.transpose(local_ids, (1, 0, 2, 3)), blocks, group, rounds)


def window_gather(extended, corner_nodes, span):
    local_ids, blocks, group, rounds = window_layout(corner_nodes, span)
    pieces = extended.reshape(3, blocks + 1, span)
    windows = jnp.concatenate([pieces[:, :-1], pieces[:, 1:]], axis=2)
    parts = jnp.transpose(split_parts(windows).reshape(9, rounds, group, 2 * span), (1, 0, 2, 3))
    window_iota = jnp.arange(2 * span, dtype=jnp.int32)

    def pick_round(items):
        part, ids = items
        onehot = (ids[..., None] == window_iota).astype(jnp.bfloat16)
        return jnp.einsum("abij,kbj->kabi", onehot, part, preferred_element_type=jnp.float32)

    picked = lax.map(pick_round, (parts, local_ids))
    picked = jnp.transpose(picked, (1, 2, 0, 3, 4)).reshape(3, 3, 4, blocks * span)
    return picked.sum(axis=0)


def window_put(corner_force, corner_nodes, span):
    local_ids, blocks, group, rounds = window_layout(corner_nodes, span)
    parts = jnp.transpose(
        split_parts(corner_force).reshape(9, 4, rounds, group, span), (2, 0, 1, 3, 4)
    )
    window_iota = jnp.arange(2 * span, dtype=jnp.int32)

    def put_round(items):
        part, ids = items
        onehot = (ids[..., None] == window_iota).astype(jnp.bfloat16)
        return jnp.einsum("abij,kabi->kbj", onehot, part, preferred_element_type=jnp.float32)

    sums = lax.map(put_round, (parts, local_ids))
    sums = jnp.transpose(sums, (1, 0, 2, 3)).reshape(3, 3, blocks, 2 * span).sum(axis=0)
    near_half = jnp.pad(sums[:, :, :span], ((0, 0), (0, 1), (0, 0)))
    far_half = jnp.pad(sums[:, :, span:], ((0, 0), (1, 0), (0, 0)))
    return (near_half + far_half).reshape(3, (blocks + 1) * span)


def spread_tiles(node_force, facet_share, tile_nodes, tile_facets, total):
    corner_share = jnp.broadcast_to(facet_share[:, None], (3, 4) + facet_share.shape[1:])
    values = jnp.concatenate([node_force.reshape(3, -1), corner_share.reshape(3, -1)], axis=1)
    index = jnp.concatenate([tile_nodes.reshape(-1), tile_facets.reshape(-1)], axis=0)
    return put_rows(values, index, total)


def ship_out(positions, velocities):
    recv_pos, recv_vel = (
        lax.all_to_all(positions, ("wid", "dep"), split_axis=1, concat_axis=1, tiled=True),
        lax.all_to_all(velocities, ("wid", "dep"), split_axis=1, concat_axis=1, tiled=True),
    )
    return (recv_pos.reshape(3, -1), recv_vel.reshape(3, -1))


def ship_back(buffer, capacity):
    group_size = lax.axis_size("wid") * lax.axis_size("dep")
    returned = lax.all_to_all(
        buffer.reshape(3, group_size, capacity),
        ("wid", "dep"),
        split_axis=1,
        concat_axis=1,
        tiled=True,
    )
    return returned


def contact_buffer(recv_pos, recv_vel, tile_nodes, tile_facets, pair_mask, live_tiles):
    total = recv_pos.shape[1]
    node_force, facet_share = tile_forces(
        recv_pos[:, tile_nodes],
        recv_vel[:, tile_nodes],
        recv_pos[:, tile_facets],
        recv_vel[:, tile_facets],
        pair_mask,
        live_tiles,
    )
    return spread_tiles(node_force, facet_share, tile_nodes, tile_facets, total)


def per_device(
    coords,
    velocity,
    node_mass,
    corner_nodes,
    shape_grad,
    frame_angles,
    volume,
    stress,
    send_nodes,
    tile_count,
    tile_nodes,
    tile_facets,
    pair_mask,
):
    axis_one, axis_two = frame_vectors(frame_angles)
    slot_rows = send_nodes[0]
    capacity = slot_rows.shape[1]
    slot_flat = slot_rows.reshape(-1)
    tile_slots = pair_mask.shape[0]
    live_tiles = (jnp.arange(tile_slots, dtype=jnp.int32) < tile_count[0]).astype(jnp.float32)
    local_count = coords.shape[1]
    for repeat in range(STEPS):
        ghosts = from_behind(velocity[:, :RIM], ("len", "wid", "dep"), -1)
        extended = jnp.concatenate([velocity, ghosts], axis=1)
        corner_vel = window_gather(extended, corner_nodes, RIM)
        corner_force, stress = element_forces(
            corner_vel, shape_grad, axis_one, axis_two, volume, stress
        )
        nodal_sum = window_put(corner_force, corner_nodes, RIM)
        returned = from_behind(nodal_sum[:, local_count:], ("len", "wid", "dep"), 1)
        internal = nodal_sum[:, :local_count] + jnp.pad(returned, ((0, 0), (0, local_count - RIM)))
        recv_pos, recv_vel = ship_out(coords[:, slot_rows], velocity[:, slot_rows])
        buffer = contact_buffer(recv_pos, recv_vel, tile_nodes, tile_facets, pair_mask, live_tiles)
        answer = ship_back(buffer, capacity)
        contact = put_rows(answer.reshape(3, -1), slot_flat, local_count)
        velocity = velocity + TIME_STEP * (internal + contact) / node_mass
        coords = coords + TIME_STEP * velocity
    return (coords, velocity, stress)


def solution(mesh):
    placed = (
        P(None, ("len", "wid", "dep")),
        P(None, ("len", "wid", "dep")),
        P(("len", "wid", "dep")),
        P(None, ("len", "wid", "dep")),
        P(None, ("len", "wid", "dep")),
        P(None, ("len", "wid", "dep")),
        P(("len", "wid", "dep")),
        P(None, ("len", "wid", "dep")),
        P(("len", "wid", "dep"), None, None),
        P(("len", "wid", "dep")),
        P(("len", "wid", "dep"), None),
        P(None, ("len", "wid", "dep"), None),
        P(("len", "wid", "dep"), None, None),
    )
    return jax.shard_map(
        per_device,
        mesh=mesh,
        in_specs=placed,
        out_specs=(
            P(None, ("len", "wid", "dep")),
            P(None, ("len", "wid", "dep")),
            P(None, ("len", "wid", "dep")),
        ),
        check_vma=False,
    )
```

profile of v0, /device:TPU:0, one launch (start us, length us, event | category | flops | bytes accessed | tf_op | source)
XLA Modules:
  0.0 197.0 jit_solution(1197763720123110898)
XLA Ops:
  2.4 10.8 %gather_fusion = f32[4096,3]{1,0:T(8,128)S(1)} fusion(f32[3,1024]{0,1:T(8,128)S(1)} %copy.159, s32[4096]{0:T(1024)S(1)} %broadcast_clamp_fusion), kind=kCustom, calls=%fused_computation | custom fusion | bytes 114688 | tf_op jit(solution)/shard_map/gather | solution.py:260
  13.2 1.2 copy.160
  14.5 7.4 %all-to-all-start = ((f32[3,16,256]{2,0,1:T(4,128)}), f32[3,16,256]{2,0,1:T(4,128)S(1)}, u32[]{:S(2)}, u32[]{:S(2)}) async-start(f32[3,16,256]{2,0,1:T(4,128)} %bitcast.19), calls=%async_computation | async-start | bytes 131072 | tf_op jit(solution)/shard_map/all_to_all | solution.py:197
  21.9 5.3 %collective-permute-start = (f32[3,128]{1,0:T(4,128)S(1)}, f32[3,128]{1,0:T(4,128)S(1)}, u32[]{:S(2)}, u32[]{:S(2)}) collective-permute-start(f32[3,128]{1,0:T(4,128)S(1)} %slice.69), channel_id=1, source_target_pairs={{0,31},{1,0},{2,1},{3,2},{4,3},{5,4},{6,5},{7,6},{8,7},{9,8},{10,9... | collective-permute-start | bytes 4616 | tf_op jit(solution)/shard_map/ppermute | solution.py:24
  30.5 10.8 %gather_fusion.3 = f32[4096,3]{1,0:T(8,128)S(1)} fusion(f32[3,1024]{0,1:T(8,128)S(1)} %copy.166, s32[4096]{0:T(1024)S(1)} %broadcast_clamp_fusion), kind=kCustom, calls=%fused_computation.3 | custom fusion | bytes 114688 | tf_op jit(solution)/shard_map/gather | solution.py:260
  41.3 1.2 copy.167
  42.7 1.4 fusion.100
  45.3 1.4 fusion.102
  47.4 3.5 %all-to-all-start.1 = ((f32[3,16,256]{2,0,1:T(4,128)}), f32[3,16,256]{2,0,1:T(4,128)S(1)}, u32[]{:S(2)}, u32[]{:S(2)}) async-start(f32[3,16,256]{2,0,1:T(4,128)} %bitcast.29), calls=%async_computation.1 | async-start | bytes 131072 | tf_op jit(solution)/shard_map/all_to_all | solution.py:198
  51.6 5.5 %gather_fusion.2 = f32[2048,3]{1,0:T(8,128)S(1)} fusion(f32[3,4096]{0,1:T(8,128)S(1)} %bitcast.286, s32[2048]{0:T(1024)S(1)} %broadcast_clamp_fusion.1), kind=kCustom, calls=%fused_computation.2 | custom fusion | bytes 57344 | tf_op jit(solution)/shard_map/gather | solution.py:220
  57.1 1.8 gather_fusion.1
  61.1 1.6 gather_fusion.4
  62.7 5.5 %gather_fusion.5 = f32[2048,3]{1,0:T(8,128)S(1)} fusion(f32[3,4096]{0,1:T(8,128)S(1)} %bitcast.291, s32[2048]{0:T(1024)S(1)} %broadcast_clamp_fusion.1), kind=kCustom, calls=%fused_computation.5 | custom fusion | bytes 57344 | tf_op jit(solution)/shard_map/gather | solution.py:221
  68.2 1.1 copy.163
  69.3 1.8 fusion.202
  71.0 1.1 copy.170
  74.5 8.7 %while.68 = (s32[]{:T(128)}, f32[9,32,128]{2,1,0:T(8,128)S(1)}, s32[5,512]{1,0:T(8,128)}, bf16[5,9,512]{2,1,0:T(8,128)(2,1)S(1)}, s32[]{:T(128)}, /*index=5*/s32[]{:T(128)}) while((s32[]{:T(128)}, f32[9,32,128]{2,1,0:T(8,128)S(1)}, s32[5,512]{1,0:T(8,128)}, bf16[5,9,512]{2,1,0:T(8,128)(2,1)S(1)}, s32[]{:T(128)}, ...), condition=%wide.region_15.16_spmd.clone, body=%wide.region_14.15_spmd.clone.sunk | while | flops 38503936 | bytes 468063 | solution.py:136
  83.9 6.0 %all-to-all-start.2 = ((f32[3,16,256]{2,0,1:T(4,128)}), f32[3,16,256]{2,0,1:T(4,128)S(1)}, u32[]{:S(2)}, u32[]{:S(2)}) async-start(f32[3,16,256]{2,0,1:T(4,128)} %bitcast.39), calls=%async_computation.2 | async-start | bytes 131072 | tf_op jit(solution)/shard_map/all_to_all | solution.py:205
  90.4 6.4 %all-to-all-done.2 = f32[3,16,256]{2,0,1:T(4,128)S(1)} async-done(((f32[3,16,256]{2,0,1:T(4,128)}), f32[3,16,256]{2,0,1:T(4,128)S(1)}, u32[]{:S(2)}, u32[]{:S(2)}) %all-to-all-start.2) | async-done | bytes 49184 | tf_op jit(solution)/shard_map/all_to_all | solution.py:205
  97.1 6.7 %while.69 = (s32[]{:T(128)}, f32[9,8,128]{2,1,0:T(8,128)S(1)}, s32[4,1024]{1,0:T(4,128)S(1)}, bf16[4,9,1024]{2,1,0:T(8,128)(2,1)S(1)}, s32[]{:T(128)}, /*index=5*/s32[]{:T(128)}) while((s32[]{:T(128)}, f32[9,8,128]{2,1,0:T(8,128)S(1)}, s32[4,1024]{1,0:T(4,128)S(1)}, bf16[4,9,1024]{2,1,0:T(8,128)(2,1)S(1)}, s32[]{:T(128)}, ...), condition=%wide.region_18.19_spmd.clone, body=%wide.region_17.18_spmd.clone.sunk | while | flops 20231172 | bytes 419935 | solution.py:136
  97.4 1.4 fusion.235
  99.1 1.4 fusion.235
  100.7 1.4 fusion.235
  102.4 1.4 fusion.235
  104.8 10.8 %gather_fusion.6 = f32[4096,3]{1,0:T(8,128)S(1)} fusion(f32[3,1024]{0,1:T(8,128)S(1)} %copy.182, s32[4096]{0:T(1024)S(1)} %broadcast_clamp_fusion), kind=kCustom, calls=%fused_computation.6 | custom fusion | bytes 114688 | tf_op jit(solution)/shard_map/gather | solution.py:260
  115.6 1.2 copy.183
  116.8 3.7 %all-to-all-start.3 = ((f32[3,16,256]{2,0,1:T(4,128)}), f32[3,16,256]{2,0,1:T(4,128)S(1)}, u32[]{:S(2)}, u32[]{:S(2)}) async-start(f32[3,16,256]{2,0,1:T(4,128)} %bitcast.58), calls=%async_computation.3 | async-start | bytes 131072 | tf_op jit(solution)/shard_map/all_to_all | solution.py:197
  120.5 10.8 %gather_fusion.9 = f32[4096,3]{1,0:T(8,128)S(1)} fusion(f32[3,1024]{0,1:T(8,128)S(1)} %copy.189, s32[4096]{0:T(1024)S(1)} %broadcast_clamp_fusion), kind=kCustom, calls=%fused_computation.9 | custom fusion | bytes 114688 | tf_op jit(solution)/shard_map/gather | solution.py:260
  131.4 1.2 copy.190
  132.7 1.4 fusion.101
  135.1 1.4 fusion.103
  137.4 6.6 %all-to-all-start.4 = ((f32[3,16,256]{2,0,1:T(4,128)}), f32[3,16,256]{2,0,1:T(4,128)S(1)}, u32[]{:S(2)}, u32[]{:S(2)}) async-start(f32[3,16,256]{2,0,1:T(4,128)} %bitcast.66), calls=%async_computation.4 | async-start | bytes 131072 | tf_op jit(solution)/shard_map/all_to_all | solution.py:198
  144.7 5.5 %gather_fusion.8 = f32[2048,3]{1,0:T(8,128)S(1)} fusion(f32[3,4096]{0,1:T(8,128)S(1)} %bitcast.292, s32[2048]{0:T(1024)S(1)} %broadcast_clamp_fusion.1), kind=kCustom, calls=%fused_computation.8 | custom fusion | bytes 57344 | tf_op jit(solution)/shard_map/gather | solution.py:220
  150.2 1.6 gather_fusion.7
  152.8 1.6 gather_fusion.10
  154.5 5.5 %gather_fusion.11 = f32[2048,3]{1,0:T(8,128)S(1)} fusion(f32[3,4096]{0,1:T(8,128)S(1)} %bitcast.289, s32[2048]{0:T(1024)S(1)} %broadcast_clamp_fusion.1), kind=kCustom, calls=%fused_computation.11 | custom fusion | bytes 57344 | tf_op jit(solution)/shard_map/gather | solution.py:221
  160.0 1.1 copy.186
  161.0 1.8 fusion.201
  162.8 1.1 copy.193
  166.2 8.7 %while.70 = (s32[]{:T(128)}, f32[9,32,128]{2,1,0:T(8,128)S(1)}, s32[5,512]{1,0:T(8,128)}, bf16[5,9,512]{2,1,0:T(8,128)(2,1)S(1)}, s32[]{:T(128)}, /*index=5*/s32[]{:T(128)}) while((s32[]{:T(128)}, f32[9,32,128]{2,1,0:T(8,128)S(1)}, s32[5,512]{1,0:T(8,128)}, bf16[5,9,512]{2,1,0:T(8,128)(2,1)S(1)}, s32[]{:T(128)}, ...), condition=%wide.region_35.36_spmd.clone, body=%wide.region_34.35_spmd.clone.sunk | while | flops 38503936 | bytes 468063 | solution.py:136
  175.7 6.0 %all-to-all-start.5 = ((f32[3,16,256]{2,0,1:T(4,128)}), f32[3,16,256]{2,0,1:T(4,128)S(1)}, u32[]{:S(2)}, u32[]{:S(2)}) async-start(f32[3,16,256]{2,0,1:T(4,128)} %bitcast.76), calls=%async_computation.5 | async-start | bytes 131072 | tf_op jit(solution)/shard_map/all_to_all | solution.py:205
  182.3 6.3 %all-to-all-done.5 = f32[3,16,256]{2,0,1:T(4,128)S(1)} async-done(((f32[3,16,256]{2,0,1:T(4,128)}), f32[3,16,256]{2,0,1:T(4,128)S(1)}, u32[]{:S(2)}, u32[]{:S(2)}) %all-to-all-start.5) | async-done | bytes 49184 | tf_op jit(solution)/shard_map/all_to_all | solution.py:205
  188.9 6.7 %while.71 = (s32[]{:T(128)}, f32[9,8,128]{2,1,0:T(8,128)S(1)}, s32[4,1024]{1,0:T(4,128)S(1)}, bf16[4,9,1024]{2,1,0:T(8,128)(2,1)S(1)}, s32[]{:T(128)}, /*index=5*/s32[]{:T(128)}) while((s32[]{:T(128)}, f32[9,8,128]{2,1,0:T(8,128)S(1)}, s32[4,1024]{1,0:T(4,128)S(1)}, bf16[4,9,1024]{2,1,0:T(8,128)(2,1)S(1)}, s32[]{:T(128)}, ...), condition=%wide.region_38.39_spmd.clone, body=%wide.region_37.38_spmd.clone.sunk | while | flops 20231172 | bytes 419935 | solution.py:136
  189.2 1.4 fusion.241
  190.9 1.4 fusion.241
  192.5 1.4 fusion.241
  194.2 1.4 fusion.241
  195.7 1.3 multiply_add_fusion
  (323 shorter events, 39.8 us)
Async XLA Ops:
  0.6 29.0 %copy-start.14 = (s32[1,16,256]{2,1,0:T(8,128)S(1)}, s32[1,16,256]{2,1,0:T(8,128)}, u32[]{:S(2)}) copy-start(s32[1,16,256]{2,1,0:T(8,128)} %param.31) | copy-start | bytes 49156
  0.6 21.2 %copy-start.1 = (f32[3,1024]{1,0:T(4,128)S(1)}, f32[3,1024]{1,0:T(4,128)}, u32[]{:S(2)}) copy-start(f32[3,1024]{1,0:T(4,128)} %param.24) | copy-start | bytes 36868
  0.7 26.6 %copy-start.28 = (s32[4,4,128]{2,1,0:T(4,128)S(1)}, s32[4,4,128]{2,1,0:T(4,128)}, u32[]{:S(2)}) copy-start(s32[4,4,128]{2,1,0:T(4,128)} %param.34) | copy-start | bytes 24580
  0.7 26.6 %copy-start.38 = (s32[4,128]{1,0:T(4,128)S(1)}, s32[4,128]{1,0:T(4,128)}, u32[]{:S(2)}) copy-start(s32[4,128]{1,0:T(4,128)} %param.33) | copy-start | bytes 6148
  0.7 27.8 %copy-start.37 = (f32[2,1024]{1,0:T(2,128)S(1)}, f32[2,1024]{1,0:T(2,128)}, u32[]{:S(2)}) copy-start(f32[2,1024]{1,0:T(2,128)} %param.28) | copy-start | bytes 24580
  0.7 28.1 %copy-start.39 = (f32[1024]{0:T(1024)S(1)}, f32[1024]{0:T(1024)}, u32[]{:S(2)}) copy-start(f32[1024]{0:T(1024)} %param.29) | copy-start | bytes 12292
  0.7 28.1 %copy-start.33 = (s32[4,1024]{1,0:T(4,128)S(1)}, s32[4,1024]{1,0:T(4,128)}, u32[]{:S(2)}) copy-start(s32[4,1024]{1,0:T(4,128)} %param.26) | copy-start | bytes 49156
  14.5 33.0 %all-to-all-start = ((f32[3,16,256]{2,0,1:T(4,128)}), f32[3,16,256]{2,0,1:T(4,128)S(1)}, u32[]{:S(2)}, u32[]{:S(2)}) async-start(f32[3,16,256]{2,0,1:T(4,128)} %bitcast.19), calls=%async_computation | async-start | bytes 131072 | tf_op jit(solution)/shard_map/all_to_all | solution.py:197
  21.9 20.7 %collective-permute-start = (f32[3,128]{1,0:T(4,128)S(1)}, f32[3,128]{1,0:T(4,128)S(1)}, u32[]{:S(2)}, u32[]{:S(2)}) collective-permute-start(f32[3,128]{1,0:T(4,128)S(1)} %slice.69), channel_id=1, source_target_pairs={{0,31},{1,0},{2,1},{3,2},{4,3},{5,4},{6,5},{7,6},{8,7},{9,8},{10,9... | collective-permute-start | bytes 4616 | tf_op jit(solution)/shard_map/ppermute | solution.py:24
  29.0 16.1 %copy-start.3 = (f32[3,1024]{1,0:T(4,128)}, f32[3,1024]{1,0:T(4,128)S(1)}, u32[]{:S(2)}) copy-start(f32[3,1024]{1,0:T(4,128)S(1)} %pad_maximum_fusion.10) | copy-start | bytes 36868
  29.1 16.0 %copy-start.7 = (f32[3,1024]{1,0:T(4,128)}, f32[3,1024]{1,0:T(4,128)S(1)}, u32[]{:S(2)}) copy-start(f32[3,1024]{1,0:T(4,128)S(1)} %maximum_maximum_fusion) | copy-start | bytes 36868
  41.3 3.0 %copy-start = (f32[8,1024]{1,0:T(8,128)S(1)}, f32[8,1024]{1,0:T(8,128)}, u32[]{:S(2)}) copy-start(f32[8,1024]{1,0:T(8,128)} %param.27) | copy-start | bytes 98308
  41.3 3.1 %copy-start.36 = (f32[3,1024]{1,0:T(4,128)S(1)}, f32[3,1024]{1,0:T(4,128)}, u32[]{:S(2)}) copy-start(f32[3,1024]{1,0:T(4,128)} %param.30) | copy-start | bytes 36868
  41.3 3.1 %copy-start.41 = (f32[4]{0:T(128)S(1)}, f32[4]{0:T(128)}, u32[]{:S(2)}) copy-start(f32[4]{0:T(128)} %constant.306.clone) | copy-start | bytes 52
  42.6 4.2 %copy-start.34 = (s32[4,8,128]{2,0,1:T(4,128)}, s32[4,8,128]{2,0,1:T(4,128)S(1)}, u32[]{:S(2)}) copy-start(s32[4,8,128]{2,0,1:T(4,128)S(1)} %copy.155) | copy-start | bytes 49156
  47.4 13.0 %all-to-all-start.1 = ((f32[3,16,256]{2,0,1:T(4,128)}), f32[3,16,256]{2,0,1:T(4,128)S(1)}, u32[]{:S(2)}, u32[]{:S(2)}) async-start(f32[3,16,256]{2,0,1:T(4,128)} %bitcast.29), calls=%async_computation.1 | async-start | bytes 131072 | tf_op jit(solution)/shard_map/all_to_all | solution.py:198
  57.1 3.9 %copy-start.17 = (s32[1024]{0:T(1024)S(1)}, s32[1024]{0:T(1024)}, u32[]{:S(2)}) copy-start(s32[1024]{0:T(1024)} %pad_clamp_fusion) | copy-start | bytes 12292
  61.1 11.3 %copy-start.27 = (f32[4,128,3]{1,2,0:T(4,128)S(1)}, f32[4,128,3]{1,2,0:T(4,128)}, u32[]{:S(2)}) copy-start(f32[4,128,3]{1,2,0:T(4,128)} %copy.172) | copy-start | bytes 18436
  72.1 2.3 %copy-start.10 = (f32[9,32,128]{2,1,0:T(8,128)S(1)}, f32[9,32,128]{2,1,0:T(8,128)}, u32[]{:S(2)}) copy-start(f32[9,32,128]{2,1,0:T(8,128)} %custom-call) | copy-start | bytes 442372
  74.4 15.5 %copy-start.15 = (f32[3,8,128]{2,1,0:T(8,128)S(1)}, f32[3,8,128]{2,1,0:T(8,128)}, u32[]{:S(2)}) copy-start(f32[3,8,128]{2,1,0:T(8,128)} %get-tuple-element.600) | copy-start | bytes 36868
  74.5 15.5 %copy-start.16 = (f32[3,8,128]{2,1,0:T(8,128)S(1)}, f32[3,8,128]{2,1,0:T(8,128)}, u32[]{:S(2)}) copy-start(f32[3,8,128]{2,1,0:T(8,128)} %get-tuple-element.601) | copy-start | bytes 36868
  74.5 22.6 %copy-start.26 = (f32[9,8,128]{2,1,0:T(8,128)S(1)}, f32[9,8,128]{2,1,0:T(8,128)}, u32[]{:S(2)}) copy-start(f32[9,8,128]{2,1,0:T(8,128)} %custom-call.1) | copy-start | bytes 110596
  83.9 12.9 %all-to-all-start.2 = ((f32[3,16,256]{2,0,1:T(4,128)}), f32[3,16,256]{2,0,1:T(4,128)S(1)}, u32[]{:S(2)}, u32[]{:S(2)}) async-start(f32[3,16,256]{2,0,1:T(4,128)} %bitcast.39), calls=%async_computation.2 | async-start | bytes 131072 | tf_op jit(solution)/shard_map/all_to_all | solution.py:205
  90.0 13.9 %collective-permute-start.1 = (f32[3,128]{1,0:T(4,128)S(1)}, f32[3,128]{1,0:T(4,128)S(1)}, u32[]{:S(2)}, u32[]{:S(2)}) collective-permute-start(f32[3,128]{1,0:T(4,128)S(1)} %slice.115), channel_id=1, source_target_pairs={{0,1},{1,2},{2,3},{3,4},{4,5},{5,6},{6,7},{7,8},{8,9},{9,10},{10,1... | collective-permute-start | bytes 4616 | tf_op jit(solution)/shard_map/ppermute | solution.py:24
  97.1 6.8 %copy-start.2 = (f32[3,1024]{1,0:T(4,128)S(1)}, f32[3,1024]{1,0:T(4,128)}, u32[]{:S(2)}) copy-start(f32[3,1024]{1,0:T(4,128)} %param.24) | copy-start | bytes 36868
  97.1 6.8 %copy-start.13 = (f32[3,1024]{1,0:T(4,128)S(1)}, f32[3,1024]{1,0:T(4,128)}, u32[]{:S(2)}) copy-start(f32[3,1024]{1,0:T(4,128)} %param.23) | copy-start | bytes 36868
  97.1 6.8 %copy-start.31 = (f32[1024]{0:T(1024)S(1)}, f32[1024]{0:T(1024)}, u32[]{:S(2)}) copy-start(f32[1024]{0:T(1024)} %param.25) | copy-start | bytes 12292
  103.9 27.4 %copy-start.5 = (f32[3,1024]{1,0:T(4,128)}, f32[3,1024]{1,0:T(4,128)S(1)}, u32[]{:S(2)}) copy-start(f32[3,1024]{1,0:T(4,128)S(1)} %get-tuple-element.584) | copy-start | bytes 36868
  103.9 28.7 %collective-permute-start.2 = (f32[3,128]{1,0:T(4,128)S(1)}, f32[3,128]{1,0:T(4,128)S(1)}, u32[]{:S(2)}, u32[]{:S(2)}) collective-permute-start(f32[3,128]{1,0:T(4,128)S(1)} %slice.116), channel_id=1, source_target_pairs={{0,31},{1,0},{2,1},{3,2},{4,3},{5,4},{6,5},{7,6},{8,7},{9,8},{10,9... | collective-permute-start | bytes 4616 | tf_op jit(solution)/shard_map/ppermute | solution.py:24
  115.6 17.1 %copy-start.35 = (s32[4,8,128]{2,0,1:T(4,128)S(1)}, s32[4,8,128]{2,0,1:T(4,128)}, u32[]{:S(2)}) copy-start(s32[4,8,128]{2,0,1:T(4,128)} %copy-done.34) | copy-start | bytes 49156
  116.8 20.5 %all-to-all-start.3 = ((f32[3,16,256]{2,0,1:T(4,128)}), f32[3,16,256]{2,0,1:T(4,128)S(1)}, u32[]{:S(2)}, u32[]{:S(2)}) async-start(f32[3,16,256]{2,0,1:T(4,128)} %bitcast.58), calls=%async_computation.3 | async-start | bytes 131072 | tf_op jit(solution)/shard_map/all_to_all | solution.py:197
  131.3 3.0 %copy-start.4 = (f32[3,1024]{1,0:T(4,128)S(1)}, f32[3,1024]{1,0:T(4,128)}, u32[]{:S(2)}) copy-start(f32[3,1024]{1,0:T(4,128)} %copy-done.3) | copy-start | bytes 36868
  131.3 3.0 %copy-start.8 = (f32[3,1024]{1,0:T(4,128)S(1)}, f32[3,1024]{1,0:T(4,128)}, u32[]{:S(2)}) copy-start(f32[3,1024]{1,0:T(4,128)} %copy-done.7) | copy-start | bytes 36868
  131.3 3.1 %copy-start.20 = (f32[1,1024]{1,0:T(1,128)S(1)}, f32[1,1024]{1,0:T(1,128)}, u32[]{:S(2)}) copy-start(f32[1,1024]{1,0:T(1,128)} %copy-done.19) | copy-start | bytes 12292
  131.3 3.1 %copy-start.22 = (f32[1,1024]{1,0:T(1,128)S(1)}, f32[1,1024]{1,0:T(1,128)}, u32[]{:S(2)}) copy-start(f32[1,1024]{1,0:T(1,128)} %copy-done.21) | copy-start | bytes 12292
  131.3 3.2 %copy-start.30 = (f32[4,1024]{1,0:T(4,128)S(1)}, f32[4,1024]{1,0:T(4,128)}, u32[]{:S(2)}) copy-start(f32[4,1024]{1,0:T(4,128)} %copy-done.29) | copy-start | bytes 49156
  131.4 3.2 %copy-start.42 = (f32[4]{0:T(128)S(1)}, f32[4]{0:T(128)}, u32[]{:S(2)}) copy-start(f32[4]{0:T(128)} %constant.306.clone) | copy-start | bytes 52
  135.1 15.0 %copy-start.18 = (s32[1024]{0:T(1024)S(1)}, s32[1024]{0:T(1024)}, u32[]{:S(2)}) copy-start(s32[1024]{0:T(1024)} %pad_clamp_fusion) | copy-start | bytes 12292
  136.7 15.5 %copy-start.11 = (f32[1,3,9,128]{3,1,2,0:T(4,128)}, f32[1,3,9,128]{3,1,2,0:T(4,128)S(1)}, u32[]{:S(2)}) copy-start(f32[1,3,9,128]{3,1,2,0:T(4,128)S(1)} %copy.229) | copy-start | bytes 41476
  137.3 58.4 %collective-permute-start.3 = (f32[3,128]{1,0:T(4,128)}, f32[3,128]{1,0:T(4,128)}, u32[]{:S(2)}, u32[]{:S(2)}) collective-permute-start(f32[3,128]{1,0:T(4,128)} %slice.122), channel_id=1, source_target_pairs={{0,1},{1,2},{2,3},{3,4},{4,5},{5,6},{6,7},{7,8},{8,9},{9,10},{10,1... | collective-permute-start | bytes 4616 | tf_op jit(solution)/shard_map/ppermute | solution.py:24
  137.4 14.8 %all-to-all-start.4 = ((f32[3,16,256]{2,0,1:T(4,128)}), f32[3,16,256]{2,0,1:T(4,128)S(1)}, u32[]{:S(2)}, u32[]{:S(2)}) async-start(f32[3,16,256]{2,0,1:T(4,128)} %bitcast.66), calls=%async_computation.4 | async-start | bytes 131072 | tf_op jit(solution)/shard_map/all_to_all | solution.py:198
  151.8 9.2 %copy-start.40 = (f32[4]{0:T(128)S(1)}, f32[4]{0:T(128)}, u32[]{:S(2)}) copy-start(f32[4]{0:T(128)} %compare_convert_fusion) | copy-start | bytes 52
  166.2 15.5 %copy-start.24 = (f32[1,1024]{1,0:T(1,128)S(1)}, f32[1,1024]{1,0:T(1,128)}, u32[]{:S(2)}) copy-start(f32[1,1024]{1,0:T(1,128)} %copy-done.23) | copy-start | bytes 12292
  166.2 22.6 %copy-start.25 = (f32[9,8,128]{2,1,0:T(8,128)S(1)}, f32[9,8,128]{2,1,0:T(8,128)}, u32[]{:S(2)}) copy-start(f32[9,8,128]{2,1,0:T(8,128)} %custom-call.3) | copy-start | bytes 110596
  175.7 12.9 %all-to-all-start.5 = ((f32[3,16,256]{2,0,1:T(4,128)}), f32[3,16,256]{2,0,1:T(4,128)S(1)}, u32[]{:S(2)}, u32[]{:S(2)}) async-start(f32[3,16,256]{2,0,1:T(4,128)} %bitcast.76), calls=%async_computation.5 | async-start | bytes 131072 | tf_op jit(solution)/shard_map/all_to_all | solution.py:205
  188.9 6.8 %copy-start.6 = (f32[3,1024]{1,0:T(4,128)S(1)}, f32[3,1024]{1,0:T(4,128)}, u32[]{:S(2)}) copy-start(f32[3,1024]{1,0:T(4,128)} %copy-done.5) | copy-start | bytes 36868
  188.9 6.8 %copy-start.12 = (f32[1,3,9,128]{3,1,2,0:T(4,128)S(1)}, f32[1,3,9,128]{3,1,2,0:T(4,128)}, u32[]{:S(2)}) copy-start(f32[1,3,9,128]{3,1,2,0:T(4,128)} %copy-done.11) | copy-start | bytes 41476
  188.9 6.8 %copy-start.32 = (f32[1024]{0:T(1024)S(1)}, f32[1024]{0:T(1024)}, u32[]{:S(2)}) copy-start(f32[1024]{0:T(1024)} %param.25) | copy-start | bytes 12292
  (5 other events, 4.7 us)
where the time goes:
time: 199 us; the launch traced here: 197 us
  local copies, waits for them, and re-layouts  97.6 us (49%)
  starting transfers between devices  39.5 us (20%)
  matrix products  32.1 us (16%)
  waiting for transfers between devices  12.7 us (6%)
  other arithmetic  11.6 us (6%)
  between operations  2.76 us (1%)
    gather x8, local copies, waits for them, and re-layouts, per_device(): recv_pos, recv_vel = ship_out(coords[:, slot_rows], velocity[:, slot_rows])  48 us
    dot_general x18, matrix products, add_block(): jnp.einsum('mh,kml->khl', high_match, spread_rows, preferred_element_type...  19.3 us
    all_to_all x2, waiting for transfers between devices, ship_back(): lax.all_to_all(buffer.reshape(3, group_size, capacity), ('wid', 'dep'), s...  12.6 us
    all_to_all x2, starting transfers between devices, ship_back(): lax.all_to_all(buffer.reshape(3, group_size, capacity), ('wid', 'dep'), s...  12 us
    all_to_all x2, starting transfers between devices, ship_out(): lax.all_to_all(positions, ('wid', 'dep'), split_axis=1, concat_axis=1, ti...  11.1 us
    gather x2, local copies, waits for them, and re-layouts, contact_buffer(): recv_pos[:, tile_facets]  10.9 us
    gather x2, local copies, waits for them, and re-layouts, contact_buffer(): recv_vel[:, tile_facets]  10.9 us
    all_to_all x2, starting transfers between devices, ship_out(): lax.all_to_all(velocities, ('wid', 'dep'), split_axis=1, concat_axis=1, t...  10.1 us
  transfers between devices with their start and end apart: 10, of which 2 were waited for; matrix products, arithmetic and copies ran while one was open for 52% of the time, Pallas kernels for 0%

commit v1 on v0

v1 whole, which is shorter than its diff:
```python
import functools

import jax
import jax.numpy as jnp
from jax import lax
from jax.experimental import pallas as pl
from jax.experimental.pallas import tpu as pltpu
from jax.sharding import PartitionSpec as P

STEPS = 2
TIME_STEP = 0.1
YOUNG_MOD = 1.0
POISSON = 0.3
HOURGLASS = 0.1
RADIUS_SQ = 1.0
STIFFNESS = 0.1
DAMPING = 0.05

LANES = 128
OUT_ROWS = 12
BACK_ROWS = 6
MESH = pl.DeviceIdType.MESH
F32 = jnp.float32
BF16 = jnp.bfloat16


def two_parts(values):
    first = values.astype(BF16)
    return first, (values - first.astype(F32)).astype(BF16)


def lane_take(table, low):
    return jnp.take_along_axis(table, low, axis=1, mode="promise_in_bounds")


def nt_dot(left, right):
    return lax.dot_general(left, right, (((1,), (1,)), ((), ())), preferred_element_type=F32)


def nn_dot(left, right):
    return lax.dot_general(left, right, (((1,), (0,)), ((), ())), preferred_element_type=F32)


def kernel(
    sizes,
    coords_in, velocity_in, mass_in, corner_in, grad_in, angles_in, volume_in, stress_in,
    send_in, count_in, nodes_in, facets_in, mask_in,
    coords_out, velocity_out, stress_out,
    pos, vel, corner, grad, stress, angle, slot_ids, tile_ids, win_hot, tile_hot, node_hot,
    win_rows, tile_lhs, node_lhs,
    send_buf, recv_buf, back_buf, answer_buf, ghost_send, ghost_recv, rim_send, rim_recv,
    out_send_sem, out_recv_sem, back_send_sem, back_recv_sem, edge_send_sem, edge_recv_sem,
):
    n_len, n_wid, n_dep = sizes
    group = n_wid * n_dep
    devices = n_len * group
    rows = coords_in.shape[1] // LANES
    halves = send_in.shape[2] // LANES
    tiles = nodes_in.shape[0]
    my_len = lax.axis_index("len")
    my_place = lax.axis_index("wid") * n_dep + lax.axis_index("dep")
    my_id = my_len * group + my_place

    def by_id(p):
        return (p // group, (p % group) // n_dep, p % n_dep)

    def partner(d):
        g = lax.rem(my_place + d, group)
        return g, (my_len, g // n_dep, lax.rem(g, n_dep))

    before = by_id(lax.rem(my_id + devices - 1, devices))
    after = by_id(lax.rem(my_id + 1, devices))

    barrier = pltpu.get_barrier_semaphore()
    for d in range(1, group):
        pl.semaphore_signal(barrier, inc=1, device_id=partner(d)[1], device_id_type=MESH)
    pl.semaphore_signal(barrier, inc=1, device_id=before, device_id_type=MESH)
    pl.semaphore_signal(barrier, inc=1, device_id=after, device_id_type=MESH)

    for i in range(rows):
        cols = pl.ds(i * LANES, LANES)
        pos[pl.ds(i, 3, stride=rows), :] = coords_in[:, cols]
        for k in range(3):
            vel[pl.ds(k * 2 * rows + i, 1), :] = velocity_in[pl.ds(k, 1), cols]
        stress[pl.ds(i, 3, stride=rows), :] = stress_in[:, cols]
        corner[pl.ds(i, 4, stride=rows), :] = corner_in[:, cols]
        grad[pl.ds(i, 8, stride=rows), :] = grad_in[:, cols]
        angle[pl.ds(i, 2, stride=rows), :] = angles_in[:, cols]
    tile_rows = tile_ids.shape[0]
    tile_ids[...] = jnp.zeros_like(tile_ids)
    tile_ids[pl.ds(0, tiles), :] = nodes_in[...]
    for a in range(4):
        tile_ids[pl.ds((a + 1) * tiles, tiles), :] = facets_in[a]

    def velocity_rows(k):
        return vel[pl.ds(k * 2 * rows, rows), :]

    def edge_copy(step, which):
        src, dst, target = ((ghost_send, ghost_recv, before), (rim_send, rim_recv, after))[which]
        return pltpu.make_async_remote_copy(
            src_ref=src.at[step], dst_ref=dst.at[step],
            send_sem=edge_send_sem.at[step, which], recv_sem=edge_recv_sem.at[step, which],
            device_id=target, device_id_type=MESH,
        )

    def group_copy(step, d, back):
        g, target = partner(d)
        if back:
            src, dst, ss, rs, n = back_buf, answer_buf, back_send_sem, back_recv_sem, BACK_ROWS
        else:
            src, dst, ss, rs, n = send_buf, recv_buf, out_send_sem, out_recv_sem, OUT_ROWS
        return pltpu.make_async_remote_copy(
            src_ref=src.at[step, g], dst_ref=dst.at[step, my_place],
            send_sem=ss.at[step, d - 1], recv_sem=rs.at[step, d - 1],
            device_id=target, device_id_type=MESH,
        )

    def fill_ghosts(step):
        for k in range(3):
            ghost_send[step, pl.ds(k, 1), :] = vel[pl.ds(k * 2 * rows, 1), :]

    def fill_slots(step):
        tables = [pos[pl.ds(k * rows, rows), :] for k in range(3)]
        tables += [velocity_rows(k) for k in range(3)]
        for half in range(halves):
            ids = send_in[0, :, pl.ds(half * LANES, LANES)]
            low, high = ids & (LANES - 1), ids >> 7
            for c in range(6):
                found = jnp.zeros(ids.shape, F32)
                for h in range(rows):
                    row = jnp.broadcast_to(tables[c][h : h + 1], ids.shape)
                    found = jnp.where(high == h, lane_take(row, low), found)
                send_buf[step, :, c * halves + half, :] = found

    fill_ghosts(0)
    fill_slots(0)
    pl.semaphore_wait(barrier, group + 1)

    sub = lax.broadcasted_iota(jnp.int32, (LANES, LANES), 0)
    for step in range(STEPS):
        edge_copy(step, 0).start()
        for d in range(1, group):
            group_copy(step, d, False).start()
        recv_buf[step, my_place] = send_buf[step, my_place]

        if step == 0:
            first_row = lax.broadcasted_iota(jnp.int32, (rows, LANES), 0) * LANES
            corner_low, corner_far = [], []
            for a in range(4):
                local = corner[pl.ds(a * rows, rows), :] - first_row
                corner_low.append(local & (LANES - 1))
                corner_far.append(local >= LANES)
                for i in range(rows):
                    hot = (sub == corner_low[a][i : i + 1]).astype(F32).astype(BF16)
                    win_hot[i, :, pl.ds(a * LANES, LANES)] = hot
            polar, azim = angle[pl.ds(0, rows), :], angle[pl.ds(rows, rows), :]
            cos_p, sin_p, cos_a, sin_a = jnp.cos(polar), jnp.sin(polar), jnp.cos(azim), jnp.sin(azim)
            one = (cos_p * cos_a, cos_p * sin_a, -sin_p)
            two = (-sin_a, cos_a)
            volume = volume_in[...]
            mass = mass_in[...]
            gx = [grad[pl.ds(a * rows, rows), :] for a in range(4)]
            gy = [grad[pl.ds((4 + a) * rows, rows), :] for a in range(4)]

        edge_copy(step, 0).wait_recv()
        for k in range(3):
            vel[pl.ds(k * 2 * rows + rows, 1), :] = ghost_recv[step, pl.ds(k, 1), :]
        corner_vel = []
        for k in range(3):
            near = velocity_rows(k)
            far = vel[pl.ds(k * 2 * rows + 1, rows), :]
            corner_vel.append([
                jnp.where(corner_far[a], lane_take(far, corner_low[a]), lane_take(near, corner_low[a]))
                for a in range(4)
            ])
        xx = yy = xy = jnp.zeros((rows, LANES), F32)
        for a in range(4):
            u = sum(one[k] * corner_vel[k][a] for k in range(3))
            w = sum(two[k] * corner_vel[k][a] for k in range(2))
            xx += gx[a] * u
            yy += gy[a] * w
            xy += gy[a] * u + gx[a] * w
        factor = TIME_STEP * YOUNG_MOD / (1.0 - POISSON * POISSON)
        sxx = stress[pl.ds(0, rows), :] + factor * (xx + POISSON * yy)
        syy = stress[pl.ds(rows, rows), :] + factor * (POISSON * xx + yy)
        sxy = stress[pl.ds(2 * rows, rows), :] + factor * 0.5 * (1.0 - POISSON) * xy
        stress[pl.ds(0, rows), :] = sxx
        stress[pl.ds(rows, rows), :] = syy
        stress[pl.ds(2 * rows, rows), :] = sxy
        hour = [
            HOURGLASS * volume
            * (corner_vel[k][0] - corner_vel[k][1] + corner_vel[k][2] - corner_vel[k][3])
            for k in range(3)
        ]
        for a in range(4):
            f1 = -volume * (gx[a] * sxx + gy[a] * sxy)
            f2 = -volume * (gy[a] * syy + gx[a] * sxy)
            for k in range(3):
                force = one[k] * f1 - (1.0 if a % 2 == 0 else -1.0) * hour[k]
                if k < 2:
                    force += two[k] * f2
                first = force.astype(BF16).astype(F32)
                for part, value in enumerate((first, force - first)):
                    for side in range(2):
                        keep = corner_far[a] if side else jnp.logical_not(corner_far[a])
                        win_rows[a, pl.ds(part * 8 + k * 2 + side, rows, stride=16), :] = jnp.where(
                            keep, value, 0.0
                        )
        for i in range(rows):
            left = jnp.concatenate(
                [win_rows[a, pl.ds(i * 16, 16), :].astype(BF16) for a in range(4)], axis=1
            )
            summed = nt_dot(left, win_hot[i])
            rim_send[step, pl.ds(i * 8, 8), :] = summed[:8] + summed[8:]
        edge = pltpu.make_async_remote_copy(
            src_ref=rim_send.at[step, pl.ds((rows - 1) * 8, 8)], dst_ref=rim_recv.at[step],
            send_sem=edge_send_sem.at[step, 1], recv_sem=edge_recv_sem.at[step, 1],
            device_id=after, device_id_type=MESH,
        )
        edge.start()

        if step == 0:
            for b in range(5 * tiles):
                low = tile_ids[pl.ds(b, 1), :] & (LANES - 1)
                tile_hot[:, pl.ds(b * LANES, LANES)] = (sub == low).astype(F32).astype(BF16)
            for g in range(group):
                for half in range(halves):
                    low = send_in[0, pl.ds(g, 1), pl.ds(half * LANES, LANES)] & (LANES - 1)
                    node_hot[:, pl.ds((g * halves + half) * LANES, LANES)] = (
                        (sub == low).astype(F32).astype(BF16)
                    )
            ids = tile_ids[...]
            ids_low, ids_high = ids & (LANES - 1), ids >> 7

        for d in range(1, group):
            group_copy(step, d, False).wait_recv()
        state = [jnp.zeros(ids.shape, F32) for c in range(6)]
        for g in range(group):
            for half in range(halves):
                match = ids_high == g * halves + half
                for c in range(6):
                    row = jnp.broadcast_to(
                        recv_buf[step, g, pl.ds(c * halves + half, 1), :], ids.shape
                    )
                    state[c] = jnp.where(match, lane_take(row, ids_low), state[c])
        centre = [
            0.25 * sum(s[(a + 1) * tiles : (a + 2) * tiles] for a in range(4)) for s in state
        ]
        nodes = [s[:tiles] for s in state]
        node_mix = [STIFFNESS * nodes[k] - DAMPING * nodes[3 + k] for k in range(3)]
        facet_mix = [STIFFNESS * centre[k] - DAMPING * centre[3 + k] for k in range(3)]
        lead = jnp.concatenate(nodes[:3] + [jnp.zeros((16 - 3 * tiles % 16, LANES), F32)], axis=0)
        columns = jnp.transpose(lead)
        ones = jnp.ones((1, LANES), F32)
        blank = jnp.zeros((4, LANES), F32)
        node_force = [[None] * tiles for k in range(3)]
        facet_force = [[None] * tiles for k in range(3)]
        for t in range(tiles):
            live = jnp.where(t < count_in[0], 1.0, 0.0)
            dist = jnp.zeros((LANES, LANES), F32)
            for k in range(3):
                gap = columns[:, k * tiles + t : k * tiles + t + 1] - centre[k][t : t + 1]
                dist += gap * gap
            weight = mask_in[t].astype(F32) * (live * jnp.maximum(RADIUS_SQ - dist, 0.0))
            w1, w2 = two_parts(weight)
            a1, a2 = two_parts(jnp.concatenate([m[t : t + 1] for m in node_mix] + [ones, blank], axis=0))
            b1, b2 = two_parts(jnp.concatenate([m[t : t + 1] for m in facet_mix] + [ones, blank], axis=0))
            left_a = jnp.concatenate([a1, a2], axis=0)
            left_b = jnp.concatenate([b1, b2], axis=0)
            to_facet = nn_dot(
                jnp.concatenate([left_a, left_a], axis=1), jnp.concatenate([w1, w2], axis=0)
            )
            to_node = nt_dot(
                jnp.concatenate([left_b, left_b], axis=1), jnp.concatenate([w1, w2], axis=1)
            )
            to_facet = to_facet[:8] + to_facet[8:]
            to_node = to_node[:8] + to_node[8:]
            for k in range(3):
                node_force[k][t] = node_mix[k][t : t + 1] * to_node[3:4] - to_node[k : k + 1]
                facet_force[k][t] = -0.25 * (
                    to_facet[k : k + 1] - to_facet[3:4] * facet_mix[k][t : t + 1]
                )
        spans = halves * group
        high_iota = lax.broadcasted_iota(jnp.int32, (spans, LANES), 0)
        for b in range(5 * tiles):
            high = ids_high[b : b + 1]
            match = high_iota == (high % halves) * group + high // halves
            for k in range(3):
                row = node_force[k][b] if b < tiles else facet_force[k][b % tiles]
                chosen = jnp.where(match, jnp.broadcast_to(row, match.shape), 0.0)
                p1, p2 = two_parts(chosen)
                cols = pl.ds(b * LANES, LANES)
                tile_lhs[pl.ds(k * spans, spans), cols] = p1
                tile_lhs[pl.ds((3 + k) * spans, spans), cols] = p2
        slots = nt_dot(tile_lhs[...], tile_hot[...])
        slots = slots[: 3 * spans] + slots[3 * spans :]
        for r in range(3 * halves):
            back_buf[step, :, r, :] = slots[r * group : (r + 1) * group]
        for d in range(1, group):
            group_copy(step, d, True).start()
        answer_buf[step, my_place] = back_buf[step, my_place]
        edge.wait_recv()
        internal = []
        for k in range(3):
            near = rim_send[step, pl.ds(k * 2, rows, stride=8), :]
            far = rim_send[step, pl.ds(k * 2 + 1, rows - 1, stride=8), :]
            edge_row = rim_recv[step, pl.ds(k * 2 + 1, 1), :]
            internal.append(near + jnp.concatenate([edge_row, far], axis=0))
        for d in range(1, group):
            group_copy(step, d, True).wait_recv()
        row_iota = lax.broadcasted_iota(jnp.int32, (rows, LANES), 0)
        for g in range(group):
            for half in range(halves):
                high = send_in[0, pl.ds(g, 1), pl.ds(half * LANES, LANES)] >> 7
                match = row_iota == high
                chosen = jnp.concatenate([
                    jnp.where(
                        match,
                        jnp.broadcast_to(answer_buf[step, g, pl.ds(k * halves + half, 1), :], match.shape),
                        0.0,
                    )
                    for k in range(3)
                ], axis=0)
                first = chosen.astype(BF16).astype(F32)
                both = jnp.concatenate([first, chosen - first], axis=0).astype(BF16)
                node_lhs[:, pl.ds((g * halves + half) * LANES, LANES)] = both
        contact = nt_dot(node_lhs[...], node_hot[...])
        contact = contact[: 3 * rows] + contact[3 * rows :]
        for k in range(3):
            fresh = velocity_rows(k) + TIME_STEP * (
                internal[k] + contact[k * rows : (k + 1) * rows]
            ) / mass
            vel[pl.ds(k * 2 * rows, rows), :] = fresh
            pos[pl.ds(k * rows, rows), :] = pos[pl.ds(k * rows, rows), :] + TIME_STEP * fresh
        if step + 1 < STEPS:
            fill_ghosts(step + 1)
            fill_slots(step + 1)

    for i in range(rows):
        cols = pl.ds(i * LANES, LANES)
        coords_out[:, cols] = pos[pl.ds(i, 3, stride=rows), :]
        velocity_out[:, cols] = vel[pl.ds(i, 3, stride=2 * rows), :]
        stress_out[:, cols] = stress[pl.ds(i, 3, stride=rows), :]
    for step in range(STEPS):
        edge_copy(step, 0).wait_send()
        pltpu.make_async_remote_copy(
            src_ref=rim_send.at[step, pl.ds((rows - 1) * 8, 8)], dst_ref=rim_recv.at[step],
            send_sem=edge_send_sem.at[step, 1], recv_sem=edge_recv_sem.at[step, 1],
            device_id=after, device_id_type=MESH,
        ).wait_send()
        for d in range(1, group):
            group_copy(step, d, False).wait_send()
            group_copy(step, d, True).wait_send()


def per_device(
    sizes, coords, velocity, node_mass, corner_nodes, shape_grad, frame_angles, volume, stress,
    send_nodes, tile_count, tile_nodes, tile_facets, pair_mask,
):
    count = coords.shape[1]
    rows = count // LANES
    group = sizes[1] * sizes[2]
    cap = send_nodes.shape[2]
    tiles = tile_nodes.shape[0]
    spans = group * cap // LANES
    vmem = pl.BlockSpec(memory_space=pltpu.VMEM)
    smem = pl.BlockSpec(memory_space=pltpu.SMEM)
    state = jax.ShapeDtypeStruct((3, count), F32)
    dma = pltpu.SemaphoreType.DMA
    return pl.pallas_call(
        functools.partial(kernel, sizes),
        out_shape=(state, state, state),
        in_specs=[vmem] * 9 + [smem] + [vmem] * 3,
        out_specs=(vmem, vmem, vmem),
        scratch_shapes=[
            pltpu.VMEM((3 * rows, LANES), F32),
            pltpu.VMEM((6 * rows, LANES), F32),
            pltpu.VMEM((4 * rows, LANES), jnp.int32),
            pltpu.VMEM((8 * rows, LANES), F32),
            pltpu.VMEM((3 * rows, LANES), F32),
            pltpu.VMEM((2 * rows, LANES), F32),
            pltpu.VMEM((8, LANES), jnp.int32),
            pltpu.VMEM((-(-5 * tiles // 8) * 8, LANES), jnp.int32),
            pltpu.VMEM((rows, LANES, 4 * LANES), BF16),
            pltpu.VMEM((LANES, 5 * tiles * LANES), BF16),
            pltpu.VMEM((LANES, group * cap), BF16),
            pltpu.VMEM((4, 16 * rows, LANES), F32),
            pltpu.VMEM((6 * spans, 5 * tiles * LANES), BF16),
            pltpu.VMEM((6 * rows, group * cap), BF16),
            pltpu.VMEM((STEPS, group, OUT_ROWS, LANES), F32),
            pltpu.VMEM((STEPS, group, OUT_ROWS, LANES), F32),
            pltpu.VMEM((STEPS, group, BACK_ROWS, LANES), F32),
            pltpu.VMEM((STEPS, group, BACK_ROWS, LANES), F32),
            pltpu.VMEM((STEPS, 3, LANES), F32),
            pltpu.VMEM((STEPS, 3, LANES), F32),
            pltpu.VMEM((STEPS, 8 * rows, LANES), F32),
            pltpu.VMEM((STEPS, 8, LANES), F32),
            dma((STEPS, group - 1)),
            dma((STEPS, group - 1)),
            dma((STEPS, group - 1)),
            dma((STEPS, group - 1)),
            dma((STEPS, 2)),
            dma((STEPS, 2)),
        ],
        compiler_params=pltpu.CompilerParams(collective_id=0, has_side_effects=True),
    )(
        coords, velocity, node_mass.reshape(rows, LANES), corner_nodes, shape_grad, frame_angles,
        volume.reshape(rows, LANES), stress, send_nodes, tile_count, tile_nodes, tile_facets, pair_mask,
    )


def solution(mesh):
    axes = ("len", "wid", "dep")
    flat, wide = P(axes), P(None, axes)
    sizes = tuple(mesh.shape[name] for name in axes)
    return jax.shard_map(
        functools.partial(per_device, sizes),
        mesh=mesh,
        in_specs=(
            wide, wide, flat, wide, wide, wide, flat, wide,
            P(axes, None, None), flat, P(axes, None), P(None, axes, None), P(axes, None, None),
        ),
        out_specs=(wide, wide, wide),
        check_vma=False,
    )
```

time: 199 us -> 37.9 us (0.19)
  local copies, waits for them, and re-layouts: 97.6 us -> 2.66 us
  starting transfers between devices: 39.5 us -> 0 us
  Pallas kernels: 0 us -> 33.6 us
  matrix products: 32.1 us -> 0 us
  waiting for transfers between devices: 12.7 us -> 0 us
  other arithmetic: 11.6 us -> 0 us
    gather x20 -> x0, local copies, waits for them, and re-layouts: 80.9 us -> none  [the longest x8 48 us: per_device(): recv_pos, recv_vel = ship_out(coords[:, slot_rows], velocity[:, slot_rows])]
    pallas_call x0 -> x1, Pallas kernels: none -> 33.6 us  [per_device(): pl.pallas_call(functools.partial(kernel, sizes), out_shape=(state, state,...]
    all_to_all x6 -> x0, starting transfers between devices: 33.2 us -> none  [the longest x2 12 us: ship_back(): lax.all_to_all(buffer.reshape(3, group_size, capacity), ('wid', 'dep'), s...]
    dot_general x32 -> x0, matrix products: 32.1 us -> none  [the longest x18 19.3 us: add_block(): jnp.einsum('mh,kml->khl', high_match, spread_rows, preferred_element_type...]
    all_to_all x6 -> x0, waiting for transfers between devices: 12.7 us -> none  [the longest x2 12.6 us: ship_back(): lax.all_to_all(buffer.reshape(3, group_size, capacity), ('wid', 'dep'), s...]
    dynamic_slice x18 -> x0, local copies, waits for them, and re-layouts: 7.35 us -> none  [put_rows(): lax.scan(add_block, jnp.zeros((3 * chans, high_span, low_span), jnp.float...]
    ppermute x4 -> x0, starting transfers between devices: 6.28 us -> none  [from_behind(): return lax.ppermute(value, axis, pairs)]
    eq x18 -> x0, other arithmetic: 2.99 us -> none  [add_block(): low_match = ids[:, None] % low_span == low_iota[None, :]]
  transfers between devices with their start and end apart: 10 -> 0, of which waited for: 2 -> 0; matrix products, arithmetic and copies ran while one was open for 52% -> 0% of each run, Pallas kernels for 0% -> 0%
where the time goes in v1:
time: 37.9 us; the launch traced here: 37.5 us
  Pallas kernels  33.6 us (89%)
  local copies, waits for them, and re-layouts  2.66 us (7%)
  between operations  1.3 us (3%)
    pallas_call x1, Pallas kernels, per_device(): pl.pallas_call(functools.partial(kernel, sizes), out_shape=(state, state,...  33.6 us
    unnamed x7, local copies, waits for them, and re-layouts  2.66 us

profile of v1, /device:TPU:0, one launch (start us, length us, event | category | flops | bytes accessed | tf_op | source)
XLA Modules:
  0.0 37.5 jit_solution(3723590178821284853)
XLA Ops:
  1.3 33.6 %shard_map.148 = (f32[3,1024]{1,0:T(4,128)}, f32[3,1024]{1,0:T(4,128)}, f32[3,1024]{1,0:T(4,128)}) custom-call(f32[3,1024]{1,0:T(4,128)} %coords_in.1, f32[3,1024]{1,0:T(4,128)} %velocity_in.1, f32[8,128]{1,0:T(8,128)} %bitcast.2, s32[4,1024]{1,0:T(4,128)} %corner_in.1, f32[8,1024]{1,0:T(8,128)} %grad_in.1, f32[2,1024]{1,0:T(2,128)} %angles_in.1, ...), custom_call_target="tpu_custom_call" | custom-call | tf_op jit(solution)/shard_map/pallas_call | solution.py:370
  34.9 0.0 copy-start.1
  34.9 1.3 %copy.20 = f32[3,1024]{1,0:T(4,128)} copy(f32[3,1024]{1,0:T(4,128)} %get-tuple-element.6) | data formatting | bytes 24576
  36.2 0.0 copy-done.1
  36.2 0.0 copy-start
  36.2 0.6 %copy.21 = f32[3,1024]{1,0:T(4,128)} copy(f32[3,1024]{1,0:T(4,128)S(1)} %copy-done.1) | data formatting | bytes 24576
  36.8 0.1 copy-done
  36.9 0.6 %copy.22 = f32[3,1024]{1,0:T(4,128)} copy(f32[3,1024]{1,0:T(4,128)S(1)} %copy-done) | data formatting | bytes 24576
Async XLA Ops:
  34.9 1.3 %copy-start.1 = (f32[3,1024]{1,0:T(4,128)S(1)}, f32[3,1024]{1,0:T(4,128)}, u32[]{:S(2)}) copy-start(f32[3,1024]{1,0:T(4,128)} %get-tuple-element.7) | copy-start | bytes 36868
  36.2 0.7 %copy-start = (f32[3,1024]{1,0:T(4,128)S(1)}, f32[3,1024]{1,0:T(4,128)}, u32[]{:S(2)}) copy-start(f32[3,1024]{1,0:T(4,128)} %get-tuple-element.8) | copy-start | bytes 36868

commit v2 on v1

--- a/solution.py
+++ b/solution.py
@@ -17,8 +17,6 @@
 DAMPING = 0.05
 
 LANES = 128
-OUT_ROWS = 12
-BACK_ROWS = 6
 MESH = pl.DeviceIdType.MESH
 F32 = jnp.float32
 BF16 = jnp.bfloat16
@@ -43,18 +41,21 @@
 
 def kernel(
     sizes,
+    coords_hbm, velocity_hbm, mass_hbm, corner_hbm, grad_hbm, angles_hbm, volume_hbm, stress_hbm,
+    send_hbm, count_in, nodes_hbm, facets_hbm, mask_hbm,
+    coords_out, velocity_out, stress_out,
     coords_in, velocity_in, mass_in, corner_in, grad_in, angles_in, volume_in, stress_in,
-    send_in, count_in, nodes_in, facets_in, mask_in,
-    coords_out, velocity_out, stress_out,
-    pos, vel, corner, grad, stress, angle, slot_ids, tile_ids, win_hot, tile_hot, node_hot,
+    send_in, nodes_in, facets_in, mask_in, in_sem,
+    pos, vel, corner, grad, stress, angle, slot_high, tile_ids, win_hot, tile_hot, node_hot,
     win_rows, tile_lhs, node_lhs,
-    send_buf, recv_buf, back_buf, answer_buf, ghost_send, ghost_recv, rim_send, rim_recv,
+    send_buf, recv_buf, again_buf, fresh_buf, back_buf, answer_buf, ghost_send, ghost_recv, rim_send, rim_recv,
     out_send_sem, out_recv_sem, back_send_sem, back_recv_sem, edge_send_sem, edge_recv_sem,
 ):
     n_len, n_wid, n_dep = sizes
     group = n_wid * n_dep
     devices = n_len * group
     rows = coords_in.shape[1] // LANES
+    order = sorted(range(1, group), key=lambda d: -min(d, group - d))
     halves = send_in.shape[2] // LANES
     tiles = nodes_in.shape[0]
     my_len = lax.axis_index("len")
@@ -71,17 +72,63 @@
     before = by_id(lax.rem(my_id + devices - 1, devices))
     after = by_id(lax.rem(my_id + 1, devices))
 
+    loads = [
+        pltpu.make_async_copy(src, dst, in_sem.at[n])
+        for n, (src, dst) in enumerate((
+            (coords_hbm, coords_in), (velocity_hbm, velocity_in), (send_hbm, send_in),
+            (corner_hbm, corner_in), (stress_hbm, stress_in), (grad_hbm, grad_in),
+            (angles_hbm, angles_in), (mass_hbm, mass_in), (volume_hbm, volume_in),
+            (nodes_hbm, nodes_in), (facets_hbm, facets_in), (mask_hbm, mask_in),
+        ))
+    ]
     barrier = pltpu.get_barrier_semaphore()
-    for d in range(1, group):
+    for d in order:
         pl.semaphore_signal(barrier, inc=1, device_id=partner(d)[1], device_id_type=MESH)
     pl.semaphore_signal(barrier, inc=1, device_id=before, device_id_type=MESH)
     pl.semaphore_signal(barrier, inc=1, device_id=after, device_id_type=MESH)
 
+    for load in loads:
+        load.start()
+    for load in loads[:3]:
+        load.wait()
     for i in range(rows):
         cols = pl.ds(i * LANES, LANES)
         pos[pl.ds(i, 3, stride=rows), :] = coords_in[:, cols]
         for k in range(3):
             vel[pl.ds(k * 2 * rows + i, 1), :] = velocity_in[pl.ds(k, 1), cols]
+
+    def velocity_rows(k):
+        return vel[pl.ds(k * 2 * rows, rows), :]
+
+    def fill_ghosts(step):
+        for k in range(3):
+            ghost_send[step, pl.ds(k, 1), :] = vel[pl.ds(k * 2 * rows, 1), :]
+
+    def fill_slots(step):
+        tables = [velocity_rows(k) for k in range(3)]
+        if step == 0:
+            tables += [pos[pl.ds(k * rows, rows), :] for k in range(3)]
+        for half in range(halves):
+            ids = send_in[0, :, pl.ds(half * LANES, LANES)]
+            low, high = ids & (LANES - 1), ids >> 7
+            if step == 0:
+                slot_high[:, half, :] = high
+            for c, table in enumerate(tables):
+                found = jnp.zeros(ids.shape, F32)
+                for h in range(rows):
+                    row = jnp.broadcast_to(table[h : h + 1], ids.shape)
+                    found = jnp.where(high == h, lane_take(row, low), found)
+                if step == 0:
+                    send_buf[:, c * halves + half, :] = found
+                else:
+                    again_buf[step - 1, :, c * halves + half, :] = found
+
+    fill_ghosts(0)
+    fill_slots(0)
+    for load in loads[3:]:
+        load.wait()
+    for i in range(rows):
+        cols = pl.ds(i * LANES, LANES)
         stress[pl.ds(i, 3, stride=rows), :] = stress_in[:, cols]
         corner[pl.ds(i, 4, stride=rows), :] = corner_in[:, cols]
         grad[pl.ds(i, 8, stride=rows), :] = grad_in[:, cols]
@@ -92,9 +139,6 @@
     for a in range(4):
         tile_ids[pl.ds((a + 1) * tiles, tiles), :] = facets_in[a]
 
-    def velocity_rows(k):
-        return vel[pl.ds(k * 2 * rows, rows), :]
-
     def edge_copy(step, which):
         src, dst, target = ((ghost_send, ghost_recv, before), (rim_send, rim_recv, after))[which]
         return pltpu.make_async_remote_copy(
@@ -106,42 +150,28 @@
     def group_copy(step, d, back):
         g, target = partner(d)
         if back:
-            src, dst, ss, rs, n = back_buf, answer_buf, back_send_sem, back_recv_sem, BACK_ROWS
+            src, dst, ss, rs = back_buf.at[step], answer_buf.at[step], back_send_sem, back_recv_sem
+        elif step == 0:
+            src, dst, ss, rs = send_buf, recv_buf, out_send_sem, out_recv_sem
         else:
-            src, dst, ss, rs, n = send_buf, recv_buf, out_send_sem, out_recv_sem, OUT_ROWS
+            src, dst, ss, rs = again_buf.at[step - 1], fresh_buf.at[step - 1], out_send_sem, out_recv_sem
         return pltpu.make_async_remote_copy(
-            src_ref=src.at[step, g], dst_ref=dst.at[step, my_place],
+            src_ref=src.at[g], dst_ref=dst.at[my_place],
             send_sem=ss.at[step, d - 1], recv_sem=rs.at[step, d - 1],
             device_id=target, device_id_type=MESH,
         )
 
-    def fill_ghosts(step):
-        for k in range(3):
-            ghost_send[step, pl.ds(k, 1), :] = vel[pl.ds(k * 2 * rows, 1), :]
-
-    def fill_slots(step):
-        tables = [pos[pl.ds(k * rows, rows), :] for k in range(3)]
-        tables += [velocity_rows(k) for k in range(3)]
-        for half in range(halves):
-            ids = send_in[0, :, pl.ds(half * LANES, LANES)]
-            low, high = ids & (LANES - 1), ids >> 7
-            for c in range(6):
-                found = jnp.zeros(ids.shape, F32)
-                for h in range(rows):
-                    row = jnp.broadcast_to(tables[c][h : h + 1], ids.shape)
-                    found = jnp.where(high == h, lane_take(row, low), found)
-                send_buf[step, :, c * halves + half, :] = found
-
-    fill_ghosts(0)
-    fill_slots(0)
     pl.semaphore_wait(barrier, group + 1)
 
     sub = lax.broadcasted_iota(jnp.int32, (LANES, LANES), 0)
     for step in range(STEPS):
         edge_copy(step, 0).start()
-        for d in range(1, group):
+        for d in order:
             group_copy(step, d, False).start()
-        recv_buf[step, my_place] = send_buf[step, my_place]
+        if step == 0:
+            recv_buf[my_place] = send_buf[my_place]
+        else:
+            fresh_buf[step - 1, my_place] = again_buf[step - 1, my_place]
 
         if step == 0:
             first_row = lax.broadcasted_iota(jnp.int32, (rows, LANES), 0) * LANES
@@ -232,17 +262,22 @@
             ids = tile_ids[...]
             ids_low, ids_high = ids & (LANES - 1), ids >> 7
 
-        for d in range(1, group):
-            group_copy(step, d, False).wait_recv()
-        state = [jnp.zeros(ids.shape, F32) for c in range(6)]
-        for g in range(group):
+        landed = recv_buf if step == 0 else fresh_buf.at[step - 1]
+        found = [jnp.zeros(ids.shape, F32) for c in range(6 if step == 0 else 3)]
+        for d in [0] + order[::-1]:
+            if d:
+                group_copy(step, d, False).wait_recv()
+            g = lax.rem(my_place + group - d, group)
             for half in range(halves):
                 match = ids_high == g * halves + half
-                for c in range(6):
-                    row = jnp.broadcast_to(
-                        recv_buf[step, g, pl.ds(c * halves + half, 1), :], ids.shape
-                    )
-                    state[c] = jnp.where(match, lane_take(row, ids_low), state[c])
+                for c in range(len(found)):
+                    row = jnp.broadcast_to(landed[g, pl.ds(c * halves + half, 1), :], ids.shape)
+                    found[c] = jnp.where(match, lane_take(row, ids_low), found[c])
+        if step == 0:
+            slot_pos = found[3:]
+        else:
+            slot_pos = [slot_pos[k] + TIME_STEP * found[k] for k in range(3)]
+        state = slot_pos + found[:3]
         centre = [
             0.25 * sum(s[(a + 1) * tiles : (a + 2) * tiles] for a in range(4)) for s in state
         ]
@@ -296,7 +331,7 @@
         slots = slots[: 3 * spans] + slots[3 * spans :]
         for r in range(3 * halves):
             back_buf[step, :, r, :] = slots[r * group : (r + 1) * group]
-        for d in range(1, group):
+        for d in order:
             group_copy(step, d, True).start()
         answer_buf[step, my_place] = back_buf[step, my_place]
         edge.wait_recv()
@@ -306,12 +341,13 @@
             far = rim_send[step, pl.ds(k * 2 + 1, rows - 1, stride=8), :]
             edge_row = rim_recv[step, pl.ds(k * 2 + 1, 1), :]
             internal.append(near + jnp.concatenate([edge_row, far], axis=0))
-        for d in range(1, group):
-            group_copy(step, d, True).wait_recv()
         row_iota = lax.broadcasted_iota(jnp.int32, (rows, LANES), 0)
-        for g in range(group):
+        for d in [0] + order[::-1]:
+            if d:
+                group_copy(step, d, True).wait_recv()
+            g = lax.rem(my_place + group - d, group)
             for half in range(halves):
-                high = send_in[0, pl.ds(g, 1), pl.ds(half * LANES, LANES)] >> 7
+                high = slot_high[g, pl.ds(half, 1), :]
                 match = row_iota == high
                 chosen = jnp.concatenate([
                     jnp.where(
@@ -323,7 +359,8 @@
                 ], axis=0)
                 first = chosen.astype(BF16).astype(F32)
                 both = jnp.concatenate([first, chosen - first], axis=0).astype(BF16)
-                node_lhs[:, pl.ds((g * halves + half) * LANES, LANES)] = both
+                start = pl.multiple_of((g * halves + half) * LANES, LANES)
+                node_lhs[:, pl.ds(start, LANES)] = both
         contact = nt_dot(node_lhs[...], node_hot[...])
         contact = contact[: 3 * rows] + contact[3 * rows :]
         for k in range(3):
@@ -336,11 +373,10 @@
             fill_ghosts(step + 1)
             fill_slots(step + 1)
 
-    for i in range(rows):
-        cols = pl.ds(i * LANES, LANES)
-        coords_out[:, cols] = pos[pl.ds(i, 3, stride=rows), :]
-        velocity_out[:, cols] = vel[pl.ds(i, 3, stride=2 * rows), :]
-        stress_out[:, cols] = stress[pl.ds(i, 3, stride=rows), :]
+    coords_out[...] = pos[...]
+    for k in range(3):
+        velocity_out[pl.ds(k * rows, rows), :] = velocity_rows(k)
+    stress_out[...] = stress[...]
     for step in range(STEPS):
         edge_copy(step, 0).wait_send()
         pltpu.make_async_remote_copy(
@@ -351,6 +387,14 @@
         for d in range(1, group):
             group_copy(step, d, False).wait_send()
             group_copy(step, d, True).wait_send()
+
+
+def arrange(coords_rows, velocity_rows, stress_rows, coords_out, velocity_out, stress_out):
+    rows = coords_rows.shape[0] // 3
+    pairs = ((coords_rows, coords_out), (velocity_rows, velocity_out), (stress_rows, stress_out))
+    for source, target in pairs:
+        for i in range(rows):
+            target[:, pl.ds(i * LANES, LANES)] = source[pl.ds(i, 3, stride=rows), :]
 
 
 def per_device(
@@ -366,20 +410,28 @@
     vmem = pl.BlockSpec(memory_space=pltpu.VMEM)
     smem = pl.BlockSpec(memory_space=pltpu.SMEM)
     state = jax.ShapeDtypeStruct((3, count), F32)
+    packed = jax.ShapeDtypeStruct((3 * rows, LANES), F32)
+    hbm = pl.BlockSpec(memory_space=pl.ANY)
+    halves = cap // LANES
+    arrays = (
+        coords, velocity, node_mass.reshape(rows, LANES), corner_nodes, shape_grad, frame_angles,
+        volume.reshape(rows, LANES), stress, send_nodes, tile_nodes, tile_facets, pair_mask,
+    )
     dma = pltpu.SemaphoreType.DMA
-    return pl.pallas_call(
+    finals = pl.pallas_call(
         functools.partial(kernel, sizes),
-        out_shape=(state, state, state),
-        in_specs=[vmem] * 9 + [smem] + [vmem] * 3,
+        out_shape=(packed, packed, packed),
+        in_specs=[hbm] * 9 + [smem] + [hbm] * 3,
         out_specs=(vmem, vmem, vmem),
-        scratch_shapes=[
+        scratch_shapes=[pltpu.VMEM(a.shape, a.dtype) for a in arrays] + [
+            dma((len(arrays),)),
             pltpu.VMEM((3 * rows, LANES), F32),
             pltpu.VMEM((6 * rows, LANES), F32),
             pltpu.VMEM((4 * rows, LANES), jnp.int32),
             pltpu.VMEM((8 * rows, LANES), F32),
             pltpu.VMEM((3 * rows, LANES), F32),
             pltpu.VMEM((2 * rows, LANES), F32),
-            pltpu.VMEM((8, LANES), jnp.int32),
+            pltpu.VMEM((group, halves, LANES), jnp.int32),
             pltpu.VMEM((-(-5 * tiles // 8) * 8, LANES), jnp.int32),
             pltpu.VMEM((rows, LANES, 4 * LANES), BF16),
             pltpu.VMEM((LANES, 5 * tiles * LANES), BF16),
@@ -387,10 +439,12 @@
             pltpu.VMEM((4, 16 * rows, LANES), F32),
             pltpu.VMEM((6 * spans, 5 * tiles * LANES), BF16),
             pltpu.VMEM((6 * rows, group * cap), BF16),
-            pltpu.VMEM((STEPS, group, OUT_ROWS, LANES), F32),
-            pltpu.VMEM((STEPS, group, OUT_ROWS, LANES), F32),
-            pltpu.VMEM((STEPS, group, BACK_ROWS, LANES), F32),
-            pltpu.VMEM((STEPS, group, BACK_ROWS, LANES), F32),
+            pltpu.VMEM((group, 6 * halves, LANES), F32),
+            pltpu.VMEM((group, 6 * halves, LANES), F32),
+            pltpu.VMEM((STEPS - 1, group, 3 * halves, LANES), F32),
+            pltpu.VMEM((STEPS - 1, group, 3 * halves, LANES), F32),
+            pltpu.VMEM((STEPS, group, 3 * halves, LANES), F32),
+            pltpu.VMEM((STEPS, group, 3 * halves, LANES), F32),
             pltpu.VMEM((STEPS, 3, LANES), F32),
             pltpu.VMEM((STEPS, 3, LANES), F32),
             pltpu.VMEM((STEPS, 8 * rows, LANES), F32),
@@ -403,10 +457,13 @@
             dma((STEPS, 2)),
         ],
         compiler_params=pltpu.CompilerParams(collective_id=0, has_side_effects=True),
-    )(
-        coords, velocity, node_mass.reshape(rows, LANES), corner_nodes, shape_grad, frame_angles,
-        volume.reshape(rows, LANES), stress, send_nodes, tile_count, tile_nodes, tile_facets, pair_mask,
-    )
+    )(*arrays[:9], tile_count, *arrays[9:])
+    return pl.pallas_call(
+        arrange,
+        out_shape=(state, state, state),
+        in_specs=[vmem] * 3,
+        out_specs=(vmem, vmem, vmem),
+    )(*finals)
 
 
 def solution(mesh):

time: 37.9 us -> 37.9 us (level)
  Pallas kernels: 33.6 us -> 36.3 us
  local copies, waits for them, and re-layouts: 2.66 us -> 0 us
    pallas_call x1 -> x2, Pallas kernels: 33.6 us -> 36.3 us  [the longest x1 34.9 us: per_device(): pl.pallas_call(functools.partial(kernel, sizes), out_shape=(packed, packe...]
    unnamed x7 -> x0, local copies, waits for them, and re-layouts: 2.66 us -> none
where the time goes in v2:
time: 37.9 us; the launch traced here: 37.6 us
  Pallas kernels  36.3 us (96%)
  between operations  1.29 us (3%)
    pallas_call x1, Pallas kernels, per_device(): pl.pallas_call(functools.partial(kernel, sizes), out_shape=(packed, packe...  34.9 us
    pallas_call x1, Pallas kernels, per_device(): pl.pallas_call(arrange, out_shape=(state, state, state), in_specs=[vmem]...  1.37 us

profile of v2, /device:TPU:0, one launch (start us, length us, event | category | flops | bytes accessed | tf_op | source)
XLA Modules:
  0.0 37.6 jit_solution(4501220585755520701)
XLA Ops:
  1.3 34.9 %shard_map.148 = (f32[24,128]{1,0:T(8,128)}, f32[24,128]{1,0:T(8,128)}, f32[24,128]{1,0:T(8,128)}) custom-call(f32[3,1024]{1,0:T(4,128)} %coords_hbm.1, f32[3,1024]{1,0:T(4,128)} %velocity_hbm.1, f32[8,128]{1,0:T(8,128)} %bitcast.2, s32[4,1024]{1,0:T(4,128)} %corner_hbm.1, f32[8,1024]{1,0:T(8,128)} %grad_hbm.1, f32[2,1024]{1,0:T(2,128)} %angles_hbm.1, ...), custom_call_target="tpu_custom_call" | custom-call | tf_op jit(solution)/shard_map/pallas_call | solution.py:421
  36.2 1.4 %shard_map.149 = (f32[3,1024]{1,0:T(4,128)}, f32[3,1024]{1,0:T(4,128)}, f32[3,1024]{1,0:T(4,128)}) custom-call(f32[24,128]{1,0:T(8,128)} %get-tuple-element.6.coords_rows, f32[24,128]{1,0:T(8,128)} %get-tuple-element.7.velocity_rows, f32[24,128]{1,0:T(8,128)} %get-tuple-element.8.stress_rows), custom_call_target="tpu_custom_call" | custom-call | tf_op jit(solution)/shard_map/pallas_call | solution.py:461

commit v3 on v2

--- a/solution.py
+++ b/solution.py
@@ -264,10 +264,9 @@
 
         landed = recv_buf if step == 0 else fresh_buf.at[step - 1]
         found = [jnp.zeros(ids.shape, F32) for c in range(6 if step == 0 else 3)]
-        for d in [0] + order[::-1]:
-            if d:
-                group_copy(step, d, False).wait_recv()
-            g = lax.rem(my_place + group - d, group)
+        for d in order[::-1]:
+            group_copy(step, d, False).wait_recv()
+        for g in range(group):
             for half in range(halves):
                 match = ids_high == g * halves + half
                 for c in range(len(found)):
@@ -342,10 +341,9 @@
             edge_row = rim_recv[step, pl.ds(k * 2 + 1, 1), :]
             internal.append(near + jnp.concatenate([edge_row, far], axis=0))
         row_iota = lax.broadcasted_iota(jnp.int32, (rows, LANES), 0)
-        for d in [0] + order[::-1]:
-            if d:
-                group_copy(step, d, True).wait_recv()
-            g = lax.rem(my_place + group - d, group)
+        for d in order[::-1]:
+            group_copy(step, d, True).wait_recv()
+        for g in range(group):
             for half in range(halves):
                 high = slot_high[g, pl.ds(half, 1), :]
                 match = row_iota == high
@@ -359,8 +357,7 @@
                 ], axis=0)
                 first = chosen.astype(BF16).astype(F32)
                 both = jnp.concatenate([first, chosen - first], axis=0).astype(BF16)
-                start = pl.multiple_of((g * halves + half) * LANES, LANES)
-                node_lhs[:, pl.ds(start, LANES)] = both
+                node_lhs[:, pl.ds((g * halves + half) * LANES, LANES)] = both
         contact = nt_dot(node_lhs[...], node_hot[...])
         contact = contact[: 3 * rows] + contact[3 * rows :]
         for k in range(3):

time: 37.9 us -> 35.4 us (0.934)
  Pallas kernels: 36.3 us -> 33.8 us
    pallas_call x1, Pallas kernels: 34.9 us -> 32.5 us  [per_device(): pl.pallas_call(functools.partial(kernel, sizes), out_shape=(packed, packe...]
where the time goes in v3:
time: 35.4 us; the launch traced here: 35.1 us
  Pallas kernels  33.8 us (95%)
  between operations  1.29 us (4%)
    pallas_call x1, Pallas kernels, per_device(): pl.pallas_call(functools.partial(kernel, sizes), out_shape=(packed, packe...  32.5 us
    pallas_call x1, Pallas kernels, per_device(): pl.pallas_call(arrange, out_shape=(state, state, state), in_specs=[vmem]...  1.37 us

profile of v3, /device:TPU:0, one launch (start us, length us, event | category | flops | bytes accessed | tf_op | source)
XLA Modules:
  0.0 35.1 jit_solution(4337531845070685619)
XLA Ops:
  1.3 32.5 %shard_map.148 = (f32[24,128]{1,0:T(8,128)}, f32[24,128]{1,0:T(8,128)}, f32[24,128]{1,0:T(8,128)}) custom-call(f32[3,1024]{1,0:T(4,128)} %coords_hbm.1, f32[3,1024]{1,0:T(4,128)} %velocity_hbm.1, f32[8,128]{1,0:T(8,128)} %bitcast.2, s32[4,1024]{1,0:T(4,128)} %corner_hbm.1, f32[8,1024]{1,0:T(8,128)} %grad_hbm.1, f32[2,1024]{1,0:T(2,128)} %angles_hbm.1, ...), custom_call_target="tpu_custom_call" | custom-call | tf_op jit(solution)/shard_map/pallas_call | solution.py:418
  33.8 1.4 %shard_map.149 = (f32[3,1024]{1,0:T(4,128)}, f32[3,1024]{1,0:T(4,128)}, f32[3,1024]{1,0:T(4,128)}) custom-call(f32[24,128]{1,0:T(8,128)} %get-tuple-element.6.coords_rows, f32[24,128]{1,0:T(8,128)} %get-tuple-element.7.velocity_rows, f32[24,128]{1,0:T(8,128)} %get-tuple-element.8.stress_rows), custom_call_target="tpu_custom_call" | custom-call | tf_op jit(solution)/shard_map/pallas_call | solution.py:458
